TPU v7x, 32 devices: a whole 2x2x4 slice. The times are simulated.
32 devices in a mesh: chan: 8 (over z, y), slot: 4 (over x, core).
Axes of the slice: x: 2, y: 2, z: 4, core: 2. Of those that a mesh axis runs over, the one named last changes fastest.
Arguments:
- visibility: float32 [2, 2, 32, 4, 3844], P(None, None, 'chan', 'slot'), parts along dimension 3, may hold values from -6 to 6
- coherency: bfloat16 [2, 2, 16, 32, 4, 3844], P(None, None, None, 'chan', 'slot'), parts along dimension 4, may hold values from -2 to 2
- jones_start: float32 [2, 2, 64, 32, 62], P(None, None, 'slot', 'chan'), parts along dimension 2, may hold values from -4 to 4
- duals_start: float32 [2, 2, 64, 32, 62], P(None, None, 'slot', 'chan'), parts along dimension 2, may hold values from -2 to 2
Outputs:
- jones_final: float32 [2, 2, 64, 32, 62], P(None, None, 'slot', 'chan'), parts along dimension 2
- consensus: float32 [2, 2, 64, 32, 62], P(None, None, 'slot', 'chan'), parts along dimension 2
- duals_final: float32 [2, 2, 64, 32, 62], P(None, None, 'slot', 'chan'), parts along dimension 2
- norms: float32 [8, 2], P('slot'), parts along dimension 0
There are 4 independent parts, one for each index of `slot`. A program takes and returns all parts, laid end to end along the dimension named above; each array names one. Nothing has to cross between parts.
All inputs are finite; a program needn't handle non-finite values.
Results may differ from a plain program's by a relative error of at most 0.0003.
Values sent between devices are 32-bit elements; how exact they have to be, the bound alone decides.
A program may use at most 128 MiB of HBM per device.

v0:
```python
import functools

import jax
import jax.numpy as jnp
from jax import lax
from jax.experimental import pallas as pl
from jax.experimental.pallas import tpu as pltpu
from jax.sharding import PartitionSpec as P

ITERS = 2
HALF = 64
BLOCK = 256
MESH = pl.DeviceIdType.MESH

penalty = 8.0
kernel_taps = (0.04, 0.06, 0.1, 0.15, 0.3, 0.15, 0.1, 0.06, 0.04)


def split(value):
    high = value.astype(jnp.bfloat16)
    return high, (value - high.astype(jnp.float32)).astype(jnp.bfloat16)


def spread_tables(width, blocks, spread_p, spread_q, gather_p):
    def fill(b, carry):
        start = pl.multiple_of(b * BLOCK, BLOCK)
        pair = (lax.broadcasted_iota(jnp.int32, (HALF, BLOCK), 1) + start).astype(jnp.float32)
        station = lax.broadcasted_iota(jnp.int32, (HALF, BLOCK), 0).astype(jnp.float32)
        first = jnp.floor((pair + 0.5) * (1.0 / width))
        second = pair - first * width
        keep = (first != second) & (first < width)
        for table, which in ((spread_p, first), (spread_q, second)):
            chosen = jnp.where((which == station) & keep, 1.0, 0.0).astype(jnp.bfloat16)
            table[0:HALF, pl.ds(start, BLOCK)] = chosen
            table[HALF:, pl.ds(start, BLOCK)] = chosen
        pair = (lax.broadcasted_iota(jnp.int32, (BLOCK, 2 * HALF), 0) + start).astype(jnp.float32)
        station = (lax.broadcasted_iota(jnp.int32, (BLOCK, 2 * HALF), 1) & (HALF - 1)).astype(jnp.float32)
        inside = pair - station * width
        keep = (inside >= 0.0) & (inside < width) & (inside != station) & (station < width)
        gather_p[pl.ds(start, BLOCK), :] = jnp.where(keep, 1.0, 0.0).astype(jnp.bfloat16)
        return carry

    lax.fori_loop(0, blocks, fill, 0)


def kernel(
    count, dims,
    vis_in, sky_in, jones_in, duals_in,
    jones_out, consensus_out, duals_out, norms_out,
    vis_raw, sky_raw, jones_raw, duals_raw,
    vis, sky, spread_p, spread_q, gather_p, lhs, left, right, parts,
    gain, cons, dual, summed, from_low, from_high, sums, slots,
    load_sem, sky_sem, send_sem, low_sem, high_sem, norm_send, norm_recv,
):
    pols, dirs, channels, width, pairs, blocks, entries = dims
    me = lax.axis_index("chan")
    group = 8 // channels
    tiles = dirs // group
    tall = tiles * 8

    loads = [
        pltpu.make_async_copy(source, target, load_sem.at[i])
        for i, (source, target) in enumerate(((vis_in, vis_raw), (jones_in, jones_raw), (duals_in, duals_raw)))
    ]
    sky_loads = [
        [pltpu.make_async_copy(sky_in.at[part, pol], sky_raw.at[part, pol], sky_sem.at[part, pol]) for part in range(2)]
        for pol in range(pols)
    ]
    for copy in loads + [copy for per_pol in sky_loads for copy in per_pol]:
        copy.start()

    from_low[...] = jnp.zeros_like(from_low)
    from_high[...] = jnp.zeros_like(from_high)
    barrier = pltpu.get_barrier_semaphore()
    for step in range(1, count):
        pl.semaphore_signal(barrier, inc=1, device_id={"chan": lax.rem(me + step, count)}, device_id_type=MESH)

    spread_tables(width, blocks, spread_p, spread_q, gather_p)
    tail = pairs // 128 * 128
    edge = blocks * BLOCK - tail
    vis[:, :, :, pl.ds(tail, edge)] = jnp.zeros((2, pols, 8, edge), jnp.float32)
    sky[:, :, :, :, pl.ds(tail, edge)] = jnp.zeros((2, pols, tiles, 8, edge), jnp.float32)
    gain[...] = jnp.zeros_like(gain)
    dual[...] = jnp.zeros_like(dual)
    sums[...] = jnp.zeros_like(sums)
    for copy in loads:
        copy.wait()
    for part in range(2):
        for pol in range(pols):
            for row in range(8):
                vis[part, pol, row : row + 1, 0:pairs] = vis_raw[part, pol, row % channels]
            for lead in range(group):
                rows = slice(lead * channels, (lead + 1) * channels)
                lanes = slice(part * HALF, part * HALF + width)
                for tile in range(tiles):
                    gain[pol, tile, rows, lanes] = jones_raw[part, pol, tile * group + lead]
                    dual[pol, tile, rows, lanes] = duals_raw[part, pol, tile * group + lead]
    cons[...] = gain[...]

    def unpack(pol):
        for copy in sky_loads[pol]:
            copy.wait()

        def one(tile, carry):
            for part in range(2):
                for lead in range(group):
                    rows = slice(lead * channels, (lead + 1) * channels)
                    sky[part, pol, tile, rows, 0:pairs] = sky_raw[part, pol, tile * group + lead].astype(jnp.float32)
            return carry

        lax.fori_loop(0, tiles, one, 0)

    def solve(pol):
        now = gain[pol].reshape(tall, 128)
        lane = lax.broadcasted_iota(jnp.int32, (tall, 128), 1)
        high = now.astype(jnp.bfloat16).astype(jnp.float32)
        low = now - high
        lhs[pol, 0:tall] = jnp.where(lane < HALF, high, pltpu.roll(low, HALF, 1)).astype(jnp.bfloat16)
        lhs[pol, tall:] = jnp.where(lane < HALF, pltpu.roll(high, HALF, 1), low).astype(jnp.bfloat16)
        right[...] = jnp.dot(lhs[pol], spread_q[...], preferred_element_type=jnp.float32)
        left[...] = jnp.dot(lhs[pol], spread_p[...], preferred_element_type=jnp.float32)

        def one_block(b, carry):
            for sub in range(0, BLOCK, 128):
                lanes = pl.ds(pl.multiple_of(b * BLOCK + sub, 128), 128)
                model_r = jnp.zeros((8, 128), jnp.float32)
                model_i = jnp.zeros((8, 128), jnp.float32)
                held = []
                for t in range(tiles):
                    sr, si = sky[0, pol, t, :, lanes], sky[1, pol, t, :, lanes]
                    mine = slice(t * 8, (t + 1) * 8)
                    other = slice(tall + t * 8, tall + (t + 1) * 8)
                    rr, ri = right[mine, lanes], right[other, lanes]
                    lr, li = left[mine, lanes], left[other, lanes]
                    zr = sr * rr + si * ri
                    zi = sr * ri - si * rr
                    model_r = model_r + (lr * zr + li * zi)
                    model_i = model_i + (li * zr - lr * zi)
                    held.append((zr, zi))
                all_r, all_i = model_r, model_i
                for lead in range(1, group):
                    all_r = all_r + pltpu.roll(model_r, lead * channels, 0)
                    all_i = all_i + pltpu.roll(model_i, lead * channels, 0)
                dr = vis[0, pol, :, lanes] - all_r
                di = vis[1, pol, :, lanes] - all_i
                for t in range(0, tiles, 2):
                    pair = held[t : t + 2]
                    values = (
                        [dr * zr - di * zi for zr, zi in pair],
                        [dr * zi + di * zr for zr, zi in pair],
                        [zr * zr + zi * zi for zr, zi in pair],
                    )
                    for i, value in enumerate(values):
                        upper, rest = split(jnp.concatenate(value, 0))
                        parts[i * tall + t * 8 : i * tall + (t + 2) * 8, lanes] = upper
                        parts[(3 + i) * tall + t * 8 : (3 + i) * tall + (t + 2) * 8, lanes] = rest
            return carry

        lax.fori_loop(0, blocks, one_block, 0)

        both = jnp.dot(parts[...], gather_p[...], preferred_element_type=jnp.float32)
        total = both[0 : 3 * tall] + both[3 * tall :]
        upper = jnp.where(lane < HALF, total[0:tall], total[tall : 2 * tall]).reshape(tiles, 8, 128)
        lower = total[2 * tall :].reshape(tiles, 8, 128)
        fresh = (upper + gain[pol] * lower + penalty * (cons[pol] - dual[pol])) / (lower + penalty)
        gain[pol] = fresh
        return fresh

    row = lax.broadcasted_iota(jnp.int32, (8, 128), 0) % channels

    def mixed(block, distance):
        out = None
        for shift in range(1 - channels, channels):
            offset = distance + shift + 4
            if offset < 0 or offset > 8:
                continue
            inside = (row + shift >= 0) & (row + shift < channels)
            weight = jnp.where(inside, kernel_taps[offset], 0.0)
            moved = block if shift == 0 else pltpu.roll(block, (-shift) % 8, 1)
            term = weight[None] * moved
            out = term if out is None else out + term
        return out

    def up_copy(it, pol):
        return pltpu.make_async_remote_copy(
            src_ref=summed.at[it, pol], dst_ref=from_low.at[it, pol],
            send_sem=send_sem.at[it, pol, 0], recv_sem=low_sem.at[it, pol],
            device_id={"chan": lax.rem(me + 1, count)}, device_id_type=MESH,
        )

    def down_copy(it, pol):
        return pltpu.make_async_remote_copy(
            src_ref=summed.at[it, pol], dst_ref=from_high.at[it, pol],
            send_sem=send_sem.at[it, pol, 1], recv_sem=high_sem.at[it, pol],
            device_id={"chan": lax.rem(me + count - 1, count)}, device_id_type=MESH,
        )

    def send(it, pol, fresh):
        summed[it, pol] = fresh + dual[pol]

        @pl.when(me < count - 1)
        def _():
            up_copy(it, pol).start()

        @pl.when(me > 0)
        def _():
            down_copy(it, pol).start()

    def smooth(it, pol):
        own = mixed(summed[it, pol], 0)

        @pl.when(me > 0)
        def _():
            up_copy(it, pol).wait_recv()

        @pl.when(me < count - 1)
        def _():
            down_copy(it, pol).wait_recv()

        fresh = own + mixed(from_low[it, pol], -channels) + mixed(from_high[it, pol], channels)
        gap = gain[pol] - fresh
        moved = fresh - cons[pol]
        dual[pol] = dual[pol] + gap
        cons[pol] = fresh
        sums[2 * it : 2 * it + 1] += jnp.sum(jnp.sum(gap * gap, 0), 0, keepdims=True)
        sums[2 * it + 1 : 2 * it + 2] += jnp.sum(jnp.sum(moved * moved, 0), 0, keepdims=True)

    def norm_copy(step):
        return pltpu.make_async_remote_copy(
            src_ref=sums, dst_ref=slots.at[me],
            send_sem=norm_send.at[step], recv_sem=norm_recv.at[step],
            device_id={"chan": lax.rem(me + step, count)}, device_id_type=MESH,
        )

    def put(target, state, pol):
        for part in range(2):
            lanes = slice(part * HALF, part * HALF + width)
            for lead in range(group):
                rows = slice(lead * channels, (lead + 1) * channels)
                for tile in range(tiles):
                    target[part, pol, tile * group + lead] = state[pol, tile, rows, lanes]

    for it in range(ITERS):
        for pol in range(pols):
            if it == 0:
                unpack(pol)
            else:
                smooth(it - 1, pol)
            fresh = solve(pol)
            if it == 0 and pol == 0:
                pl.semaphore_wait(barrier, count - 1)
            send(it, pol, fresh)
    for pol in range(pols):
        put(jones_out, gain, pol)
    for pol in range(pols):
        smooth(ITERS - 1, pol)

    slots[pl.ds(me, 1)] = sums[...][None]
    for step in range(1, count):
        norm_copy(step).start()
    for pol in range(pols):
        put(consensus_out, cons, pol)
        put(duals_out, dual, pol)

    for it in range(ITERS):
        for pol in range(pols):

            @pl.when(me < count - 1)
            def _():
                up_copy(it, pol).wait_send()

            @pl.when(me > 0)
            def _():
                down_copy(it, pol).wait_send()

    for step in range(1, count):
        norm_copy(step).wait()
    gathered = slots[0]
    for j in range(1, count):
        gathered = gathered + slots[j]
    folded = jnp.sum(gathered, axis=1, keepdims=True) * (1.0 / entries)
    for it in range(ITERS):
        norms_out[it : it + 1, 0:1] = folded[2 * it : 2 * it + 1]
        norms_out[it : it + 1, 1:2] = folded[2 * it + 1 : 2 * it + 2] * (penalty * penalty)


def solution(mesh):
    count = mesh.shape["chan"]

    def local(visibility, coherency, jones_start, duals_start):
        _, pols, dirs, channels, width = jones_start.shape
        pairs = visibility.shape[-1]
        times = visibility.shape[3]
        assert times == 1 and channels == 4 and dirs % 4 == 0 and width <= HALF - 2
        blocks = pl.cdiv(pairs, BLOCK)
        long = blocks * BLOCK
        tiles = dirs * channels // 8
        tall = tiles * 8
        entries = jones_start.size * count
        sky = coherency.transpose(0, 1, 2, 4, 3, 5).reshape(2, pols, dirs, channels, pairs)
        state = jax.ShapeDtypeStruct(jones_start.shape, jnp.float32)
        f32, bf16 = jnp.float32, jnp.bfloat16
        packed = (pols, tiles, 8, 2 * HALF)
        return pl.pallas_call(
            functools.partial(kernel, count, (pols, dirs, channels, width, pairs, blocks, entries)),
            out_shape=(state, state, state, jax.ShapeDtypeStruct((ITERS, 2), f32)),
            in_specs=[pl.BlockSpec(memory_space=pl.ANY)] * 4,
            out_specs=tuple([pl.BlockSpec(memory_space=pltpu.VMEM)] * 4),
            scratch_shapes=[
                pltpu.VMEM(visibility.shape, f32),
                pltpu.VMEM(sky.shape, bf16),
                pltpu.VMEM(jones_start.shape, f32),
                pltpu.VMEM(duals_start.shape, f32),
                pltpu.VMEM((2, pols, 8, long), f32),
                pltpu.VMEM((2, pols, tiles, 8, long), f32),
                pltpu.VMEM((2 * HALF, long), bf16),
                pltpu.VMEM((2 * HALF, long), bf16),
                pltpu.VMEM((long, 2 * HALF), bf16),
                pltpu.VMEM((pols, 2 * tall, 2 * HALF), bf16),
                pltpu.VMEM((2 * tall, long), f32),
                pltpu.VMEM((2 * tall, long), f32),
                pltpu.VMEM((6 * tall, long), bf16),
                pltpu.VMEM(packed, f32),
                pltpu.VMEM(packed, f32),
                pltpu.VMEM(packed, f32),
                pltpu.VMEM((ITERS,) + packed, f32),
                pltpu.VMEM((ITERS,) + packed, f32),
                pltpu.VMEM((ITERS,) + packed, f32),
                pltpu.VMEM((8, 2 * HALF), f32),
                pltpu.VMEM((count, 8, 2 * HALF), f32),
                pltpu.SemaphoreType.DMA((3,)),
                pltpu.SemaphoreType.DMA((2, pols)),
                pltpu.SemaphoreType.DMA((ITERS, pols, 2)),
                pltpu.SemaphoreType.DMA((ITERS, pols)),
                pltpu.SemaphoreType.DMA((ITERS, pols)),
                pltpu.SemaphoreType.DMA((count,)),
                pltpu.SemaphoreType.DMA((count,)),
            ],
            compiler_params=pltpu.CompilerParams(
                collective_id=0, has_side_effects=True, vmem_limit_bytes=60 * 1024 * 1024
            ),
        )(visibility, sky, jones_start, duals_start)

    placed = (
        P(None, None, "chan", "slot", None),
        P(None, None, None, "chan", "slot", None),
        P(None, None, "slot", "chan", None),
        P(None, None, "slot", "chan", None),
    )
    return jax.shard_map(
        local,
        mesh=mesh,
        in_specs=placed,
        out_specs=(
            P(None, None, "slot", "chan", None),
            P(None, None, "slot", "chan", None),
            P(None, None, "slot", "chan", None),
            P("slot", None),
        ),
        check_vma=False,
    )
```

profile of v0, /device:TPU:0, one launch (start us, length us, event | category | flops | bytes accessed | tf_op | source)
XLA Modules:
  0.0 40.0 jit_solution(9420234406341352010)
XLA Ops:
  0.6 33.5 %shard_map.75 = (f32[2,2,16,4,62]{4,3,2,1,0:T(4,128)}, f32[2,2,16,4,62]{4,3,2,1,0:T(4,128)}, f32[2,2,16,4,62]{4,3,2,1,0:T(4,128)}, f32[2,2]{1,0:T(2,128)}) custom-call(f32[2,2,4,1,3844]{4,3,2,1,0:T(1,128)} %vis_in.1, bf16[2,2,16,4,3844]{4,3,2,1,0:T(4,128)(2,1)} %bitcast.1, f32[2,2,16,4,62]{4,3,2,1,0:T(4,128)} %jones_in.1, f32[2,2,16,4,62]{4,3,2,1,0:T(4,128)} %duals_in.1), custom_call_target="tpu_custom_call" | custom-call | tf_op jit(solution)/shard_map/pallas_call | solution.py:304
  34.1 1.6 %copy.12 = f32[2,2,16,4,62]{4,3,2,1,0:T(4,128)} copy(f32[2,2,16,4,62]{4,3,2,1,0:T(4,128)} %get-tuple-element.8) | data formatting | bytes 126976
  35.7 1.6 %copy.13 = f32[2,2,16,4,62]{4,3,2,1,0:T(4,128)} copy(f32[2,2,16,4,62]{4,3,2,1,0:T(4,128)} %get-tuple-element.9) | data formatting | bytes 126976
  37.2 1.6 %copy.14 = f32[2,2,16,4,62]{4,3,2,1,0:T(4,128)} copy(f32[2,2,16,4,62]{4,3,2,1,0:T(4,128)} %get-tuple-element.10) | data formatting | bytes 126976
  38.8 1.2 %copy.15 = f32[2,2]{1,0:T(2,128)} copy(f32[2,2]{1,0:T(2,128)} %get-tuple-element.11) | data formatting | bytes 32
where the time goes:
time: 40.2 us; the launch traced here: 40 us
  Pallas kernels  33.5 us (83%)
  local copies, waits for them, and re-layouts  5.9 us (15%)
  between operations  0.64 us (2%)
    pallas_call x1, Pallas kernels, local(): pl.pallas_call(functools.partial(kernel, count, (pols, dirs, channels, wi...  33.5 us
    unnamed x4, local copies, waits for them, and re-layouts  5.9 us

commit v1 on v0

v1 whole, which is shorter than its diff:
```python
import functools

import jax
import jax.numpy as jnp
from jax import lax
from jax.experimental import pallas as pl
from jax.experimental.pallas import tpu as pltpu
from jax.sharding import PartitionSpec as P

ITERS = 2
PITCH = 64
GROUP = 8
CHUNKS = 2
MESH = pl.DeviceIdType.MESH

penalty = 8.0
kernel_taps = (0.04, 0.06, 0.1, 0.15, 0.3, 0.15, 0.1, 0.06, 0.04)


def kernel(
    count, dims,
    vis_in, sky_in, jones_in, duals_in,
    jones_out, consensus_out, duals_out, norms_out,
    vis_raw, sky_raw, tail_raw, jones_raw, duals_raw,
    vis_rows, base, mixer, sky, vis, z_keep, rest, acc,
    gain, cons, dual, summed, from_low, from_high, sums, slots,
    load_sem, sky_sem, tail_sem, send_sem, low_sem, high_sem, norm_send, norm_recv,
):
    pols, dirs, channels, width, pairs, entries = dims
    lanes = pols * dirs * channels
    tiles = pl.cdiv(pairs, 128)
    whole = pairs // 128
    me = lax.axis_index("chan")

    loads = [
        pltpu.make_async_copy(source, target, load_sem.at[i])
        for i, (source, target) in enumerate(((vis_in, vis_raw), (jones_in, jones_raw), (duals_in, duals_raw)))
    ]
    sky_loads = [
        pltpu.make_async_copy(sky_in.at[:, :, :, :, 128 * j : 128 * j + 128], sky_raw.at[j], sky_sem.at[j])
        for j in range(whole)
    ]
    tail_load = pltpu.make_async_copy(sky_in.at[:, :, :, :, 128 * whole : pairs], tail_raw, tail_sem)
    for copy in loads + sky_loads + [tail_load]:
        copy.start()

    from_low[...] = jnp.zeros_like(from_low)
    from_high[...] = jnp.zeros_like(from_high)
    barrier = pltpu.get_barrier_semaphore()
    for step in range(1, count):
        pl.semaphore_signal(barrier, inc=1, device_id={"chan": lax.rem(me + step, count)}, device_id_type=MESH)

    sums[...] = jnp.zeros_like(sums)
    sky_raw[whole] = jnp.zeros(sky_raw.shape[1:], sky_raw.dtype)
    sky[:, width:] = jnp.zeros((2, PITCH - width, PITCH, lanes), jnp.float32)
    vis[:, width:] = jnp.zeros((2, PITCH - width, PITCH, lanes), jnp.float32)
    vis_rows[:, :, 128 * whole :] = jnp.zeros((2, 2 * channels, 128 * (tiles - whole)), jnp.float32)
    row = lax.broadcasted_iota(jnp.int32, (2 * PITCH, 256), 0)
    col = lax.broadcasted_iota(jnp.int32, (2 * PITCH, 256), 1)
    station = row & (PITCH - 1)
    target = jnp.where(row >= PITCH, station + width, station)
    base[...] = jnp.where(station < width, col - target, -1024)
    row = lax.broadcasted_iota(jnp.int32, (2 * lanes, lanes), 0) & (lanes - 1)
    col = lax.broadcasted_iota(jnp.int32, (2 * lanes, lanes), 1)
    half = dirs * channels
    same = ((row >= half) == (col >= half)) & ((row & (channels - 1)) == (col & (channels - 1)))
    mixer[...] = jnp.where(same, -1.0, 0.0).astype(jnp.bfloat16)

    def chooser(i):
        return jnp.where(base[...] == (2 * width * i) % 128, 1.0, 0.0).astype(jnp.bfloat16)

    def swung(left, right):
        return lax.dot_general(left, right, (((1,), (1,)), ((), ())), preferred_element_type=jnp.float32)

    loads[0].wait()
    for part in range(2):
        for pol in range(pols):
            for f in range(channels):
                vis_rows[part, pol * channels + f : pol * channels + f + 1, 0:pairs] = vis_raw[part, pol, f]
    upper = lax.broadcasted_iota(jnp.int32, (2 * channels, 256), 0) < channels
    lane = lax.broadcasted_iota(jnp.int32, (2 * PITCH, lanes), 1)
    real = (lane & 8) == 0
    gap = jnp.zeros((half - 16, 256), jnp.float32)
    for i in range(width // 2):
        j = (2 * width * i) // 128
        first, second = [], []
        for part in range(2):
            value = vis_rows[part, :, 128 * j : 128 * j + 256]
            high = value.astype(jnp.bfloat16).astype(jnp.float32)
            low = pltpu.roll(value - high, channels, 0)
            first.append(jnp.where(upper, high, low))
            second.append(jnp.where(upper, low, high))
        right = jnp.concatenate(first + [gap] + second + [gap], 0).astype(jnp.bfloat16)
        turned = swung(chooser(i), right)
        vis[0, 2 * i : 2 * i + 2] = jnp.where(real, turned, 0.0).reshape(2, PITCH, lanes)
        vis[1, 2 * i : 2 * i + 2] = jnp.where(real, 0.0, turned).reshape(2, PITCH, lanes)

    for copy in loads[1:]:
        copy.wait()
    for part in range(2):
        start = jnp.transpose(jones_raw[part].reshape(lanes, width))
        gain[0, part, 0:width] = start
        cons[part, 0:width] = start
        dual[part, 0:width] = jnp.transpose(duals_raw[part].reshape(lanes, width))
        empty = jnp.zeros((PITCH - width, lanes), jnp.float32)
        gain[0, part, width:] = empty
        cons[part, width:] = empty
        dual[part, width:] = empty

    for j in range(whole):
        sky_loads[j].wait()
    tail_load.wait()
    sky_raw[whole, :, :, :, :, 0 : pairs - 128 * whole] = tail_raw[...]
    for i in range(width // 2):
        j = (2 * width * i) // 128
        right = jnp.concatenate(
            [sky_raw[j].reshape(2 * lanes, 128), sky_raw[j + 1].reshape(2 * lanes, 128)], 1
        )
        turned = swung(chooser(i), right)
        for part in range(2):
            sky[part, 2 * i : 2 * i + 2] = turned[:, part * lanes : (part + 1) * lanes].reshape(2, PITCH, lanes)
            for p in (2 * i, 2 * i + 1):
                sky[part, p, p : p + 1] = jnp.zeros((1, lanes), jnp.float32)

    def parted(value):
        high = value.astype(jnp.bfloat16)
        low = (value - high.astype(jnp.float32)).astype(jnp.bfloat16)
        return jnp.concatenate([high, low], 1)

    def sweep(it, block, carry):
        gr, gi = gain[it, 0], gain[it, 1]
        sides = ([], [])
        for b in range(GROUP):
            p = block * GROUP + b
            sr, si = sky[0, p], sky[1, p]
            zr = sr * gr + si * gi
            zi = sr * gi - si * gr
            z_keep[0, b] = zr
            z_keep[1, b] = zi
            lr, li = gain[it, 0, pl.ds(p, 1)], gain[it, 1, pl.ds(p, 1)]
            sides[0].append(parted(lr * zr + li * zi - vis[0, p]))
            sides[1].append(parted(li * zr - lr * zi - vis[1, p]))
        for part in range(2):
            rest[part] = jnp.dot(
                jnp.concatenate(sides[part], 0), mixer[...], preferred_element_type=jnp.float32
            ).reshape(GROUP, PITCH, lanes)
        sums_of = ([], [], [])
        for b in range(GROUP):
            zr, zi = z_keep[0, b], z_keep[1, b]
            dr, di = rest[0, b], rest[1, b]
            for i, value in enumerate((dr * zr - di * zi, dr * zi + di * zr, zr * zr + zi * zi)):
                sums_of[i].append(jnp.sum(value, 0, keepdims=True))
        for i in range(3):
            acc[i, pl.ds(pl.multiple_of(block * GROUP, GROUP), GROUP)] = jnp.concatenate(sums_of[i], 0)
        return carry

    tall = PITCH // CHUNKS
    place = lax.broadcasted_iota(jnp.int32, (tall, lanes), 1) & (channels - 1)

    def mixed(block, distance):
        out = None
        for shift in range(1 - channels, channels):
            offset = distance + shift + 4
            if offset < 0 or offset > 8:
                continue
            inside = (place + shift >= 0) & (place + shift < channels)
            weight = jnp.where(inside, kernel_taps[offset], 0.0)
            moved = block if shift == 0 else pltpu.roll(block, (-shift) % lanes, 1)
            term = weight * moved
            out = term if out is None else out + term
        return out

    def up_copy(it, chunk):
        return pltpu.make_async_remote_copy(
            src_ref=summed.at[it, chunk], dst_ref=from_low.at[it, chunk],
            send_sem=send_sem.at[it, chunk, 0], recv_sem=low_sem.at[it, chunk],
            device_id={"chan": lax.rem(me + 1, count)}, device_id_type=MESH,
        )

    def down_copy(it, chunk):
        return pltpu.make_async_remote_copy(
            src_ref=summed.at[it, chunk], dst_ref=from_high.at[it, chunk],
            send_sem=send_sem.at[it, chunk, 1], recv_sem=high_sem.at[it, chunk],
            device_id={"chan": lax.rem(me + count - 1, count)}, device_id_type=MESH,
        )

    def finish(it, chunk):
        rows = slice(chunk * tall, (chunk + 1) * tall)
        lower = acc[2, rows]
        scale = lower + penalty
        for part in range(2):
            goal = cons[part, rows] - dual[part, rows]
            fresh = (acc[part, rows] + gain[it, part, rows] * lower + penalty * goal) / scale
            gain[it + 1, part, rows] = fresh
            summed[it, chunk, part] = fresh + dual[part, rows]

        @pl.when(me < count - 1)
        def _():
            up_copy(it, chunk).start()

        @pl.when(me > 0)
        def _():
            down_copy(it, chunk).start()

    def smooth(it, chunk):
        rows = slice(chunk * tall, (chunk + 1) * tall)

        @pl.when(me > 0)
        def _():
            up_copy(it, chunk).wait_recv()

        @pl.when(me < count - 1)
        def _():
            down_copy(it, chunk).wait_recv()

        for part in range(2):
            fresh = (
                mixed(summed[it, chunk, part], 0)
                + mixed(from_low[it, chunk, part], -channels)
                + mixed(from_high[it, chunk, part], channels)
            )
            off = gain[it + 1, part, rows] - fresh
            moved = fresh - cons[part, rows]
            dual[part, rows] = dual[part, rows] + off
            cons[part, rows] = fresh
            sums[2 * it : 2 * it + 1] += jnp.sum(off * off, 0, keepdims=True)
            sums[2 * it + 1 : 2 * it + 2] += jnp.sum(moved * moved, 0, keepdims=True)

    def norm_copy(step):
        return pltpu.make_async_remote_copy(
            src_ref=sums, dst_ref=slots.at[me],
            send_sem=norm_send.at[step], recv_sem=norm_recv.at[step],
            device_id={"chan": lax.rem(me + step, count)}, device_id_type=MESH,
        )

    def put(target, state):
        for part in range(2):
            target[part] = jnp.transpose(state[part])[:, 0:width].reshape(pols, dirs, channels, width)

    steps = PITCH // GROUP // CHUNKS
    for it in range(ITERS):
        for chunk in range(CHUNKS):
            lax.fori_loop(chunk * steps, (chunk + 1) * steps, functools.partial(sweep, it), 0)
            if it == 0 and chunk == 0:
                pl.semaphore_wait(barrier, count - 1)
            if it > 0:
                smooth(it - 1, chunk)
            finish(it, chunk)
    put(jones_out, gain.at[ITERS])
    for chunk in range(CHUNKS):
        smooth(ITERS - 1, chunk)

    slots[pl.ds(me, 1)] = sums[...][None]
    for step in range(1, count):
        norm_copy(step).start()
    put(consensus_out, cons)
    put(duals_out, dual)

    for it in range(ITERS):
        for chunk in range(CHUNKS):

            @pl.when(me < count - 1)
            def _():
                up_copy(it, chunk).wait_send()

            @pl.when(me > 0)
            def _():
                down_copy(it, chunk).wait_send()

    for step in range(1, count):
        norm_copy(step).wait()
    gathered = slots[0]
    for j in range(1, count):
        gathered = gathered + slots[j]
    folded = jnp.sum(gathered, axis=1, keepdims=True) * (1.0 / entries)
    for it in range(ITERS):
        norms_out[it : it + 1, 0:1] = folded[2 * it : 2 * it + 1]
        norms_out[it : it + 1, 1:2] = folded[2 * it + 1 : 2 * it + 2] * (penalty * penalty)


def deliver(*refs):
    sources, targets, sem = refs[0:4], refs[4:8], refs[8]
    copies = [pltpu.make_async_copy(s, t, sem.at[i]) for i, (s, t) in enumerate(zip(sources, targets))]
    for copy in copies:
        copy.start()
    for copy in copies:
        copy.wait()


def solution(mesh):
    count = mesh.shape["chan"]

    def local(visibility, coherency, jones_start, duals_start):
        _, pols, dirs, channels, width = jones_start.shape
        pairs = visibility.shape[-1]
        times = visibility.shape[3]
        lanes = pols * dirs * channels
        assert times == 1 and pols == 2 and channels == 4 and lanes == 128 and width <= PITCH - 2 and width % 2 == 0
        tiles = pl.cdiv(pairs, 128)
        whole = pairs // 128
        entries = jones_start.size * count
        sky = coherency.transpose(0, 1, 2, 4, 3, 5).reshape(2, pols, dirs, channels, pairs)
        state = jax.ShapeDtypeStruct(jones_start.shape, jnp.float32)
        f32, bf16 = jnp.float32, jnp.bfloat16
        rows = PITCH // CHUNKS
        shapes = (state, state, state, jax.ShapeDtypeStruct((ITERS, 2), f32))
        packed = (2, PITCH, lanes)
        halo = (ITERS, CHUNKS, 2, rows, lanes)
        results = pl.pallas_call(
            functools.partial(kernel, count, (pols, dirs, channels, width, pairs, entries)),
            out_shape=shapes,
            in_specs=[pl.BlockSpec(memory_space=pl.ANY)] * 4,
            out_specs=tuple([pl.BlockSpec(memory_space=pltpu.VMEM)] * 4),
            scratch_shapes=[
                pltpu.VMEM(visibility.shape, f32),
                pltpu.VMEM((tiles, 2, pols, dirs, channels, 128), bf16),
                pltpu.VMEM((2, pols, dirs, channels, pairs - 128 * whole), bf16),
                pltpu.VMEM(jones_start.shape, f32),
                pltpu.VMEM(duals_start.shape, f32),
                pltpu.VMEM((2, 2 * channels, tiles * 128), f32),
                pltpu.VMEM((2 * PITCH, 256), jnp.int32),
                pltpu.VMEM((2 * lanes, lanes), bf16),
                pltpu.VMEM((2, PITCH, PITCH, lanes), f32),
                pltpu.VMEM((2, PITCH, PITCH, lanes), f32),
                pltpu.VMEM((2, GROUP, PITCH, lanes), f32),
                pltpu.VMEM((2, GROUP, PITCH, lanes), f32),
                pltpu.VMEM((3, PITCH, lanes), f32),
                pltpu.VMEM((ITERS + 1,) + packed, f32),
                pltpu.VMEM(packed, f32),
                pltpu.VMEM(packed, f32),
                pltpu.VMEM(halo, f32),
                pltpu.VMEM(halo, f32),
                pltpu.VMEM(halo, f32),
                pltpu.VMEM((8, lanes), f32),
                pltpu.VMEM((count, 8, lanes), f32),
                pltpu.SemaphoreType.DMA((3,)),
                pltpu.SemaphoreType.DMA((whole,)),
                pltpu.SemaphoreType.DMA,
                pltpu.SemaphoreType.DMA((ITERS, CHUNKS, 2)),
                pltpu.SemaphoreType.DMA((ITERS, CHUNKS)),
                pltpu.SemaphoreType.DMA((ITERS, CHUNKS)),
                pltpu.SemaphoreType.DMA((count,)),
                pltpu.SemaphoreType.DMA((count,)),
            ],
            compiler_params=pltpu.CompilerParams(
                collective_id=0, has_side_effects=True, vmem_limit_bytes=60 * 1024 * 1024
            ),
        )(visibility, sky, jones_start, duals_start)
        return pl.pallas_call(
            deliver,
            out_shape=shapes,
            in_specs=[pl.BlockSpec(memory_space=pl.ANY)] * 4,
            out_specs=tuple([pl.BlockSpec(memory_space=pl.ANY)] * 4),
            scratch_shapes=[pltpu.SemaphoreType.DMA((4,))],
        )(*results)

    placed = (
        P(None, None, "chan", "slot", None),
        P(None, None, None, "chan", "slot", None),
        P(None, None, "slot", "chan", None),
        P(None, None, "slot", "chan", None),
    )
    return jax.shard_map(
        local,
        mesh=mesh,
        in_specs=placed,
        out_specs=(
            P(None, None, "slot", "chan", None),
            P(None, None, "slot", "chan", None),
            P(None, None, "slot", "chan", None),
            P("slot", None),
        ),
        check_vma=False,
    )
```

time: 40.2 us -> 37.1 us (0.923)
  local copies, waits for them, and re-layouts: 5.9 us -> 0 us
  Pallas kernels: 33.5 us -> 36.3 us
    pallas_call x0 -> x1, Pallas kernels: none -> 13.1 us  [local(): pl.pallas_call(deliver, out_shape=shapes, in_specs=[pl.BlockSpec(memory_s...]
    pallas_call x1, Pallas kernels: 33.5 us -> 23.2 us  [local(): pl.pallas_call(functools.partial(kernel, count, (pols, dirs, channels, wi...]
    unnamed x4 -> x0, local copies, waits for them, and re-layouts: 5.9 us -> none
where the time goes in v1:
time: 37.1 us; the launch traced here: 37 us
  Pallas kernels  36.3 us (98%)
  between operations  0.64 us (2%)
    pallas_call x1, Pallas kernels, local(): pl.pallas_call(functools.partial(kernel, count, (pols, dirs, channels, wi...  23.2 us
    pallas_call x1, Pallas kernels, local(): pl.pallas_call(deliver, out_shape=shapes, in_specs=[pl.BlockSpec(memory_s...  13.1 us

profile of v1, /device:TPU:0, one launch (start us, length us, event | category | flops | bytes accessed | tf_op | source)
XLA Modules:
  0.0 37.0 jit_solution(7452137874969677411)
XLA Ops:
  0.6 23.2 %shard_map.75 = (f32[2,2,16,4,62]{4,3,2,1,0:T(4,128)}, f32[2,2,16,4,62]{4,3,2,1,0:T(4,128)}, f32[2,2,16,4,62]{4,3,2,1,0:T(4,128)}, f32[2,2]{1,0:T(2,128)}) custom-call(f32[2,2,4,1,3844]{4,3,2,1,0:T(1,128)} %vis_in.1, bf16[2,2,16,4,3844]{4,3,2,1,0:T(4,128)(2,1)} %bitcast.1, f32[2,2,16,4,62]{4,3,2,1,0:T(4,128)} %jones_in.1, f32[2,2,16,4,62]{4,3,2,1,0:T(4,128)} %duals_in.1), custom_call_target="tpu_custom_call" | custom-call | tf_op jit(solution)/shard_map/pallas_call | solution.py:309
  23.9 13.1 %shard_map.76 = (f32[2,2,16,4,62]{4,3,2,1,0:T(4,128)}, f32[2,2,16,4,62]{4,3,2,1,0:T(4,128)}, f32[2,2,16,4,62]{4,3,2,1,0:T(4,128)}, f32[2,2]{1,0:T(2,128)}) custom-call(f32[2,2,16,4,62]{4,3,2,1,0:T(4,128)} %get-tuple-element.8.refs_0_, f32[2,2,16,4,62]{4,3,2,1,0:T(4,128)} %get-tuple-element.9.refs_1_, f32[2,2,16,4,62]{4,3,2,1,0:T(4,128)} %get-tuple-element.10.refs_2_, ...), custom_call_target="tpu_custom_call" | custom-call | tf_op jit(solution)/shard_map/pallas_call | solution.py:349

commit v2 on v1

--- a/solution.py
+++ b/solution.py
@@ -343,15 +343,16 @@
                 pltpu.SemaphoreType.DMA((count,)),
             ],
             compiler_params=pltpu.CompilerParams(
-                collective_id=0, has_side_effects=True, vmem_limit_bytes=60 * 1024 * 1024
+                collective_id=0, has_side_effects=True, vmem_limit_bytes=24 * 1024 * 1024
             ),
-        )(visibility, sky, jones_start, duals_start)
+        )(*[pltpu.with_memory_space_constraint(x, pltpu.HBM) for x in (visibility, sky, jones_start, duals_start)])
         return pl.pallas_call(
             deliver,
             out_shape=shapes,
-            in_specs=[pl.BlockSpec(memory_space=pl.ANY)] * 4,
+            in_specs=[pl.BlockSpec(memory_space=pltpu.VMEM)] * 4,
             out_specs=tuple([pl.BlockSpec(memory_space=pl.ANY)] * 4),
             scratch_shapes=[pltpu.SemaphoreType.DMA((4,))],
+            compiler_params=pltpu.CompilerParams(vmem_limit_bytes=4 * 1024 * 1024),
         )(*results)
 
     placed = (

time: 37.1 us -> 24.1 us (0.65)
  Pallas kernels: 36.3 us -> 23.3 us
    pallas_call x1, Pallas kernels: 13.1 us -> 0.78 us  [local(): pl.pallas_call(deliver, out_shape=shapes, in_specs=[pl.BlockSpec(memory_s...]
    pallas_call x1, Pallas kernels: 23.2 us -> 22.6 us  [local(): pl.pallas_call(functools.partial(kernel, count, (pols, dirs, channels, wi...]
where the time goes in v2:
time: 24.1 us; the launch traced here: 24 us
  Pallas kernels  23.3 us (97%)
  between operations  0.64 us (3%)
    pallas_call x1, Pallas kernels, local(): pl.pallas_call(functools.partial(kernel, count, (pols, dirs, channels, wi...  22.6 us
    pallas_call x1, Pallas kernels, local(): pl.pallas_call(deliver, out_shape=shapes, in_specs=[pl.BlockSpec(memory_s...  0.78 us

profile of v2, /device:TPU:0, one launch (start us, length us, event | category | flops | bytes accessed | tf_op | source)
XLA Modules:
  0.0 24.0 jit_solution(5862995703451845553)
XLA Ops:
  0.6 22.6 %shard_map.75 = (f32[2,2,16,4,62]{4,3,2,1,0:T(4,128)S(1)}, f32[2,2,16,4,62]{4,3,2,1,0:T(4,128)S(1)}, f32[2,2,16,4,62]{4,3,2,1,0:T(4,128)S(1)}, f32[2,2]{1,0:T(2,128)S(1)}) custom-call(f32[2,2,4,1,3844]{4,3,2,1,0:T(1,128)} %vis_in.1, bf16[2,2,16,4,3844]{4,3,2,1,0:T(4,128)(2,1)} %bitcast.1, f32[2,2,16,4,62]{4,3,2,1,0:T(4,128)} %jones_in.1, ...), custom_call_target="tpu_custom_call" | custom-call | tf_op jit(solution)/shard_map/pallas_call | solution.py:309
  23.2 0.8 %shard_map.76 = (f32[2,2,16,4,62]{4,3,2,1,0:T(4,128)}, f32[2,2,16,4,62]{4,3,2,1,0:T(4,128)}, f32[2,2,16,4,62]{4,3,2,1,0:T(4,128)}, f32[2,2]{1,0:T(2,128)}) custom-call(f32[2,2,16,4,62]{4,3,2,1,0:T(4,128)S(1)} %get-tuple-element.8.refs_0_, f32[2,2,16,4,62]{4,3,2,1,0:T(4,128)S(1)} %get-tuple-element.9.refs_1_, ...), custom_call_target="tpu_custom_call" | custom-call | tf_op jit(solution)/shard_map/pallas_call | solution.py:349

commit v3 on v2

--- a/solution.py
+++ b/solution.py
@@ -10,7 +10,7 @@
 ITERS = 2
 PITCH = 64
 GROUP = 8
-CHUNKS = 2
+CHUNKS = ((0, 32), (32, 56), (56, 64))
 MESH = pl.DeviceIdType.MESH
 
 penalty = 8.0
@@ -22,8 +22,8 @@
     vis_in, sky_in, jones_in, duals_in,
     jones_out, consensus_out, duals_out, norms_out,
     vis_raw, sky_raw, tail_raw, jones_raw, duals_raw,
-    vis_rows, base, mixer, sky, vis, z_keep, rest, acc,
-    gain, cons, dual, summed, from_low, from_high, sums, slots,
+    vis_rows, chooser, mixer, sky, vis, z_keep, rest, acc,
+    gain, cons, dual, summed, from_low, from_high, sums, partial, slots,
     load_sem, sky_sem, tail_sem, send_sem, low_sem, high_sem, norm_send, norm_recv,
 ):
     pols, dirs, channels, width, pairs, entries = dims
@@ -55,45 +55,56 @@
     sky[:, width:] = jnp.zeros((2, PITCH - width, PITCH, lanes), jnp.float32)
     vis[:, width:] = jnp.zeros((2, PITCH - width, PITCH, lanes), jnp.float32)
     vis_rows[:, :, 128 * whole :] = jnp.zeros((2, 2 * channels, 128 * (tiles - whole)), jnp.float32)
-    row = lax.broadcasted_iota(jnp.int32, (2 * PITCH, 256), 0)
-    col = lax.broadcasted_iota(jnp.int32, (2 * PITCH, 256), 1)
+    row = lax.broadcasted_iota(jnp.int32, (2 * PITCH, 128), 0)
+    col = lax.broadcasted_iota(jnp.int32, (2 * PITCH, 128), 1)
     station = row & (PITCH - 1)
     target = jnp.where(row >= PITCH, station + width, station)
-    base[...] = jnp.where(station < width, col - target, -1024)
+    chooser[...] = jnp.where((station < width) & (col == target), 1.0, 0.0).astype(jnp.bfloat16)
     row = lax.broadcasted_iota(jnp.int32, (2 * lanes, lanes), 0) & (lanes - 1)
     col = lax.broadcasted_iota(jnp.int32, (2 * lanes, lanes), 1)
     half = dirs * channels
     same = ((row >= half) == (col >= half)) & ((row & (channels - 1)) == (col & (channels - 1)))
     mixer[...] = jnp.where(same, -1.0, 0.0).astype(jnp.bfloat16)
 
-    def chooser(i):
-        return jnp.where(base[...] == (2 * width * i) % 128, 1.0, 0.0).astype(jnp.bfloat16)
-
-    def swung(left, right):
-        return lax.dot_general(left, right, (((1,), (1,)), ((), ())), preferred_element_type=jnp.float32)
+    def window(first, second, i, start=None):
+        offset = (2 * width * i) % 128
+        if offset == 0:
+            return first
+        back = 128 - offset
+        lane = lax.broadcasted_iota(jnp.int32, first.shape, 1)
+        return jnp.where(lane < back, pltpu.roll(first, back, 1), pltpu.roll(second, back, 1))
+
+    def swung(right):
+        return lax.dot_general(chooser[...], right, (((1,), (1,)), ((), ())), preferred_element_type=jnp.float32)
 
     loads[0].wait()
     for part in range(2):
         for pol in range(pols):
             for f in range(channels):
                 vis_rows[part, pol * channels + f : pol * channels + f + 1, 0:pairs] = vis_raw[part, pol, f]
-    upper = lax.broadcasted_iota(jnp.int32, (2 * channels, 256), 0) < channels
+    upper = lax.broadcasted_iota(jnp.int32, (2 * channels, 128), 0) < channels
     lane = lax.broadcasted_iota(jnp.int32, (2 * PITCH, lanes), 1)
     real = (lane & 8) == 0
-    gap = jnp.zeros((half - 16, 256), jnp.float32)
-    for i in range(width // 2):
+    gap = jnp.zeros((half - 16, 128), jnp.float32)
+
+    def vis_side(i):
         j = (2 * width * i) // 128
         first, second = [], []
         for part in range(2):
-            value = vis_rows[part, :, 128 * j : 128 * j + 256]
+            value = window(vis_rows[part, :, 128 * j : 128 * j + 128], vis_rows[part, :, 128 * j + 128 : 128 * j + 256], i)
             high = value.astype(jnp.bfloat16).astype(jnp.float32)
             low = pltpu.roll(value - high, channels, 0)
             first.append(jnp.where(upper, high, low))
             second.append(jnp.where(upper, low, high))
-        right = jnp.concatenate(first + [gap] + second + [gap], 0).astype(jnp.bfloat16)
-        turned = swung(chooser(i), right)
-        vis[0, 2 * i : 2 * i + 2] = jnp.where(real, turned, 0.0).reshape(2, PITCH, lanes)
-        vis[1, 2 * i : 2 * i + 2] = jnp.where(real, 0.0, turned).reshape(2, PITCH, lanes)
+        return jnp.concatenate(first + [gap] + second + [gap], 0).astype(jnp.bfloat16)
+
+    for i in range(0, width // 2, 2):
+        both = range(i, min(i + 2, width // 2))
+        turned = swung(jnp.concatenate([vis_side(k) for k in both], 0))
+        for n, k in enumerate(both):
+            mine = turned[:, n * lanes : (n + 1) * lanes]
+            vis[0, 2 * k : 2 * k + 2] = jnp.where(real, mine, 0.0).reshape(2, PITCH, lanes)
+            vis[1, 2 * k : 2 * k + 2] = jnp.where(real, 0.0, mine).reshape(2, PITCH, lanes)
 
     for copy in loads[1:]:
         copy.wait()
@@ -107,25 +118,40 @@
         cons[part, width:] = empty
         dual[part, width:] = empty
 
-    for j in range(whole):
-        sky_loads[j].wait()
-    tail_load.wait()
-    sky_raw[whole, :, :, :, :, 0 : pairs - 128 * whole] = tail_raw[...]
-    for i in range(width // 2):
-        j = (2 * width * i) // 128
-        right = jnp.concatenate(
-            [sky_raw[j].reshape(2 * lanes, 128), sky_raw[j + 1].reshape(2 * lanes, 128)], 1
-        )
-        turned = swung(chooser(i), right)
-        for part in range(2):
-            sky[part, 2 * i : 2 * i + 2] = turned[:, part * lanes : (part + 1) * lanes].reshape(2, PITCH, lanes)
-            for p in (2 * i, 2 * i + 1):
-                sky[part, p, p : p + 1] = jnp.zeros((1, lanes), jnp.float32)
+    done = [0]
+
+    def turn(block):
+        pairs_to = range(block * GROUP // 2, min((block + 1) * GROUP // 2, width // 2))
+        last = min((2 * width * pairs_to[-1]) // 128 + 1, whole)
+        while done[0] <= last:
+            if done[0] < whole:
+                sky_loads[done[0]].wait()
+            else:
+                tail_load.wait()
+                sky_raw[whole, :, :, :, :, 0 : pairs - 128 * whole] = tail_raw[...]
+            done[0] += 1
+        for i in pairs_to:
+            j = (2 * width * i) // 128
+            turned = swung(window(sky_raw[j].reshape(2 * lanes, 128), sky_raw[j + 1].reshape(2 * lanes, 128), i))
+            for part in range(2):
+                sky[part, 2 * i : 2 * i + 2] = turned[:, part * lanes : (part + 1) * lanes].reshape(2, PITCH, lanes)
+                for p in (2 * i, 2 * i + 1):
+                    sky[part, p, p : p + 1] = jnp.zeros((1, lanes), jnp.float32)
 
     def parted(value):
         high = value.astype(jnp.bfloat16)
         low = (value - high.astype(jnp.float32)).astype(jnp.bfloat16)
         return jnp.concatenate([high, low], 1)
+
+    def gathered_rows(values):
+        row = lax.broadcasted_iota(jnp.int32, (8, lanes), 0)
+        for bit in (1, 2, 4):
+            even = (row & bit) == 0
+            values = [
+                jnp.where(even, a, b) + pltpu.roll(jnp.where(even, b, a), bit, 0)
+                for a, b in zip(values[0::2], values[1::2])
+            ]
+        return values[0]
 
     def sweep(it, block, carry):
         gr, gi = gain[it, 0], gain[it, 1]
@@ -149,13 +175,12 @@
             zr, zi = z_keep[0, b], z_keep[1, b]
             dr, di = rest[0, b], rest[1, b]
             for i, value in enumerate((dr * zr - di * zi, dr * zi + di * zr, zr * zr + zi * zi)):
-                sums_of[i].append(jnp.sum(value, 0, keepdims=True))
+                sums_of[i].append(jnp.sum(value.reshape(PITCH // 8, 8, lanes), 0))
         for i in range(3):
-            acc[i, pl.ds(pl.multiple_of(block * GROUP, GROUP), GROUP)] = jnp.concatenate(sums_of[i], 0)
+            acc[i, pl.ds(pl.multiple_of(block * GROUP, GROUP), GROUP)] = gathered_rows(sums_of[i])
         return carry
 
-    tall = PITCH // CHUNKS
-    place = lax.broadcasted_iota(jnp.int32, (tall, lanes), 1) & (channels - 1)
+    place = lax.broadcasted_iota(jnp.int32, (8, lanes), 1) & (channels - 1)
 
     def mixed(block, distance):
         out = None
@@ -164,7 +189,7 @@
             if offset < 0 or offset > 8:
                 continue
             inside = (place + shift >= 0) & (place + shift < channels)
-            weight = jnp.where(inside, kernel_taps[offset], 0.0)
+            weight = jnp.where(inside, kernel_taps[offset], 0.0)[0:1]
             moved = block if shift == 0 else pltpu.roll(block, (-shift) % lanes, 1)
             term = weight * moved
             out = term if out is None else out + term
@@ -172,27 +197,27 @@
 
     def up_copy(it, chunk):
         return pltpu.make_async_remote_copy(
-            src_ref=summed.at[it, chunk], dst_ref=from_low.at[it, chunk],
+            src_ref=summed.at[it, :, slice(*CHUNKS[chunk])], dst_ref=from_low.at[it, :, slice(*CHUNKS[chunk])],
             send_sem=send_sem.at[it, chunk, 0], recv_sem=low_sem.at[it, chunk],
             device_id={"chan": lax.rem(me + 1, count)}, device_id_type=MESH,
         )
 
     def down_copy(it, chunk):
         return pltpu.make_async_remote_copy(
-            src_ref=summed.at[it, chunk], dst_ref=from_high.at[it, chunk],
+            src_ref=summed.at[it, :, slice(*CHUNKS[chunk])], dst_ref=from_high.at[it, :, slice(*CHUNKS[chunk])],
             send_sem=send_sem.at[it, chunk, 1], recv_sem=high_sem.at[it, chunk],
             device_id={"chan": lax.rem(me + count - 1, count)}, device_id_type=MESH,
         )
 
     def finish(it, chunk):
-        rows = slice(chunk * tall, (chunk + 1) * tall)
+        rows = slice(*CHUNKS[chunk])
         lower = acc[2, rows]
         scale = lower + penalty
         for part in range(2):
             goal = cons[part, rows] - dual[part, rows]
             fresh = (acc[part, rows] + gain[it, part, rows] * lower + penalty * goal) / scale
             gain[it + 1, part, rows] = fresh
-            summed[it, chunk, part] = fresh + dual[part, rows]
+            summed[it, part, rows] = fresh + dual[part, rows]
 
         @pl.when(me < count - 1)
         def _():
@@ -203,7 +228,7 @@
             down_copy(it, chunk).start()
 
     def smooth(it, chunk):
-        rows = slice(chunk * tall, (chunk + 1) * tall)
+        rows = slice(*CHUNKS[chunk])
 
         @pl.when(me > 0)
         def _():
@@ -215,20 +240,20 @@
 
         for part in range(2):
             fresh = (
-                mixed(summed[it, chunk, part], 0)
-                + mixed(from_low[it, chunk, part], -channels)
-                + mixed(from_high[it, chunk, part], channels)
+                mixed(summed[it, part, rows], 0)
+                + mixed(from_low[it, part, rows], -channels)
+                + mixed(from_high[it, part, rows], channels)
             )
             off = gain[it + 1, part, rows] - fresh
             moved = fresh - cons[part, rows]
             dual[part, rows] = dual[part, rows] + off
             cons[part, rows] = fresh
-            sums[2 * it : 2 * it + 1] += jnp.sum(off * off, 0, keepdims=True)
-            sums[2 * it + 1 : 2 * it + 2] += jnp.sum(moved * moved, 0, keepdims=True)
+            sums[2 * it] += jnp.sum((off * off).reshape(-1, 8, lanes), 0)
+            sums[2 * it + 1] += jnp.sum((moved * moved).reshape(-1, 8, lanes), 0)
 
     def norm_copy(step):
         return pltpu.make_async_remote_copy(
-            src_ref=sums, dst_ref=slots.at[me],
+            src_ref=partial, dst_ref=slots.at[me],
             send_sem=norm_send.at[step], recv_sem=norm_recv.at[step],
             device_id={"chan": lax.rem(me + step, count)}, device_id_type=MESH,
         )
@@ -237,27 +262,43 @@
         for part in range(2):
             target[part] = jnp.transpose(state[part])[:, 0:width].reshape(pols, dirs, channels, width)
 
-    steps = PITCH // GROUP // CHUNKS
+    turn(0)
     for it in range(ITERS):
-        for chunk in range(CHUNKS):
-            lax.fori_loop(chunk * steps, (chunk + 1) * steps, functools.partial(sweep, it), 0)
+        for chunk, (start, stop) in enumerate(CHUNKS):
+            if it == 0:
+                for block in range(start // GROUP, stop // GROUP):
+                    if (block + 1) * GROUP < PITCH:
+                        turn(block + 1)
+                    sweep(it, block, 0)
+            else:
+                lax.fori_loop(start // GROUP, stop // GROUP, functools.partial(sweep, it), 0)
+                smooth(it - 1, chunk)
             if it == 0 and chunk == 0:
                 pl.semaphore_wait(barrier, count - 1)
-            if it > 0:
-                smooth(it - 1, chunk)
             finish(it, chunk)
     put(jones_out, gain.at[ITERS])
-    for chunk in range(CHUNKS):
+    for chunk in range(len(CHUNKS)):
         smooth(ITERS - 1, chunk)
 
-    slots[pl.ds(me, 1)] = sums[...][None]
+    lane = lax.broadcasted_iota(jnp.int32, (1, lanes), 1)
+    share = lanes // (2 * ITERS)
+    packed = jnp.zeros((1, lanes), jnp.float32)
+    for i in range(2 * ITERS):
+        value = jnp.sum(sums[i], 0, keepdims=True)
+        stride = lanes // 2
+        while stride >= share:
+            value = value + pltpu.roll(value, stride, 1)
+            stride //= 2
+        packed = jnp.where(lane // share == i, value, packed)
+    partial[...] = packed
+    slots[pl.ds(me, 1)] = packed[None]
     for step in range(1, count):
         norm_copy(step).start()
     put(consensus_out, cons)
     put(duals_out, dual)
 
     for it in range(ITERS):
-        for chunk in range(CHUNKS):
+        for chunk in range(len(CHUNKS)):
 
             @pl.when(me < count - 1)
             def _():
@@ -272,10 +313,10 @@
     gathered = slots[0]
     for j in range(1, count):
         gathered = gathered + slots[j]
-    folded = jnp.sum(gathered, axis=1, keepdims=True) * (1.0 / entries)
     for it in range(ITERS):
-        norms_out[it : it + 1, 0:1] = folded[2 * it : 2 * it + 1]
-        norms_out[it : it + 1, 1:2] = folded[2 * it + 1 : 2 * it + 2] * (penalty * penalty)
+        for n, factor in enumerate((1.0, penalty * penalty)):
+            mine = jnp.where(lane // share == 2 * it + n, gathered, 0.0)
+            norms_out[it : it + 1, n : n + 1] = jnp.sum(mine, axis=1, keepdims=True) * (factor / entries)
 
 
 def deliver(*refs):
@@ -302,10 +343,10 @@
         sky = coherency.transpose(0, 1, 2, 4, 3, 5).reshape(2, pols, dirs, channels, pairs)
         state = jax.ShapeDtypeStruct(jones_start.shape, jnp.float32)
         f32, bf16 = jnp.float32, jnp.bfloat16
-        rows = PITCH // CHUNKS
         shapes = (state, state, state, jax.ShapeDtypeStruct((ITERS, 2), f32))
         packed = (2, PITCH, lanes)
-        halo = (ITERS, CHUNKS, 2, rows, lanes)
+        halo = (ITERS, 2, PITCH, lanes)
+        parts = len(CHUNKS)
         results = pl.pallas_call(
             functools.partial(kernel, count, (pols, dirs, channels, width, pairs, entries)),
             out_shape=shapes,
@@ -318,7 +359,7 @@
                 pltpu.VMEM(jones_start.shape, f32),
                 pltpu.VMEM(duals_start.shape, f32),
                 pltpu.VMEM((2, 2 * channels, tiles * 128), f32),
-                pltpu.VMEM((2 * PITCH, 256), jnp.int32),
+                pltpu.VMEM((2 * PITCH, 128), bf16),
                 pltpu.VMEM((2 * lanes, lanes), bf16),
                 pltpu.VMEM((2, PITCH, PITCH, lanes), f32),
                 pltpu.VMEM((2, PITCH, PITCH, lanes), f32),
@@ -331,14 +372,15 @@
                 pltpu.VMEM(halo, f32),
                 pltpu.VMEM(halo, f32),
                 pltpu.VMEM(halo, f32),
-                pltpu.VMEM((8, lanes), f32),
-                pltpu.VMEM((count, 8, lanes), f32),
+                pltpu.VMEM((2 * ITERS, 8, lanes), f32),
+                pltpu.VMEM((1, lanes), f32),
+                pltpu.VMEM((count, 1, lanes), f32),
                 pltpu.SemaphoreType.DMA((3,)),
                 pltpu.SemaphoreType.DMA((whole,)),
                 pltpu.SemaphoreType.DMA,
-                pltpu.SemaphoreType.DMA((ITERS, CHUNKS, 2)),
-                pltpu.SemaphoreType.DMA((ITERS, CHUNKS)),
-                pltpu.SemaphoreType.DMA((ITERS, CHUNKS)),
+                pltpu.SemaphoreType.DMA((ITERS, parts, 2)),
+                pltpu.SemaphoreType.DMA((ITERS, parts)),
+                pltpu.SemaphoreType.DMA((ITERS, parts)),
                 pltpu.SemaphoreType.DMA((count,)),
                 pltpu.SemaphoreType.DMA((count,)),
             ],

time: 24.1 us -> 23.3 us (0.967)
  Pallas kernels: 23.3 us -> 22.5 us
    pallas_call x1, Pallas kernels: 22.6 us -> 21.7 us  [local(): pl.pallas_call(functools.partial(kernel, count, (pols, dirs, channels, wi...]
where the time goes in v3:
time: 23.3 us; the launch traced here: 23.1 us
  Pallas kernels  22.5 us (97%)
  between operations  0.64 us (3%)
    pallas_call x1, Pallas kernels, local(): pl.pallas_call(functools.partial(kernel, count, (pols, dirs, channels, wi...  21.7 us
    pallas_call x1, Pallas kernels, local(): pl.pallas_call(deliver, out_shape=shapes, in_specs=[pl.BlockSpec(memory_s...  0.78 us

profile of v3, /device:TPU:0, one launch (start us, length us, event | category | flops | bytes accessed | tf_op | source)
XLA Modules:
  0.0 23.1 jit_solution(7939462368723703623)
XLA Ops:
  0.6 21.7 %shard_map.75 = (f32[2,2,16,4,62]{4,3,2,1,0:T(4,128)S(1)}, f32[2,2,16,4,62]{4,3,2,1,0:T(4,128)S(1)}, f32[2,2,16,4,62]{4,3,2,1,0:T(4,128)S(1)}, f32[2,2]{1,0:T(2,128)S(1)}) custom-call(f32[2,2,4,1,3844]{4,3,2,1,0:T(1,128)} %vis_in.1, bf16[2,2,16,4,3844]{4,3,2,1,0:T(4,128)(2,1)} %bitcast.1, f32[2,2,16,4,62]{4,3,2,1,0:T(4,128)} %jones_in.1, ...), custom_call_target="tpu_custom_call" | custom-call | tf_op jit(solution)/shard_map/pallas_call | solution.py:350
  22.3 0.8 %shard_map.76 = (f32[2,2,16,4,62]{4,3,2,1,0:T(4,128)}, f32[2,2,16,4,62]{4,3,2,1,0:T(4,128)}, f32[2,2,16,4,62]{4,3,2,1,0:T(4,128)}, f32[2,2]{1,0:T(2,128)}) custom-call(f32[2,2,16,4,62]{4,3,2,1,0:T(4,128)S(1)} %get-tuple-element.8.refs_0_, f32[2,2,16,4,62]{4,3,2,1,0:T(4,128)S(1)} %get-tuple-element.9.refs_1_, ...), custom_call_target="tpu_custom_call" | custom-call | tf_op jit(solution)/shard_map/pallas_call | solution.py:391

commit v4 on v3

--- a/solution.py
+++ b/solution.py
@@ -10,6 +10,7 @@
 ITERS = 2
 PITCH = 64
 GROUP = 8
+TALL = 144
 CHUNKS = ((0, 32), (32, 56), (56, 64))
 MESH = pl.DeviceIdType.MESH
 
@@ -22,7 +23,7 @@
     vis_in, sky_in, jones_in, duals_in,
     jones_out, consensus_out, duals_out, norms_out,
     vis_raw, sky_raw, tail_raw, jones_raw, duals_raw,
-    vis_rows, chooser, mixer, sky, vis, z_keep, rest, acc,
+    vis_rows, chooser, placer, mixer, sky, vis, z_keep, rest, acc,
     gain, cons, dual, summed, from_low, from_high, sums, partial, slots,
     load_sem, sky_sem, tail_sem, send_sem, low_sem, high_sem, norm_send, norm_recv,
 ):
@@ -41,15 +42,22 @@
         for j in range(whole)
     ]
     tail_load = pltpu.make_async_copy(sky_in.at[:, :, :, :, 128 * whole : pairs], tail_raw, tail_sem)
-    for copy in loads + sky_loads + [tail_load]:
+    for copy in loads:
         copy.start()
+
+    def issue(j, carry):
+        start = pl.multiple_of(j * 128, 128)
+        pltpu.make_async_copy(sky_in.at[:, :, :, :, pl.ds(start, 128)], sky_raw.at[j], sky_sem.at[j]).start()
+        return carry
+
+    lax.fori_loop(0, whole, issue, 0)
+    tail_load.start()
 
     from_low[...] = jnp.zeros_like(from_low)
     from_high[...] = jnp.zeros_like(from_high)
     barrier = pltpu.get_barrier_semaphore()
     for step in range(1, count):
         pl.semaphore_signal(barrier, inc=1, device_id={"chan": lax.rem(me + step, count)}, device_id_type=MESH)
-
     sums[...] = jnp.zeros_like(sums)
     sky_raw[whole] = jnp.zeros(sky_raw.shape[1:], sky_raw.dtype)
     sky[:, width:] = jnp.zeros((2, PITCH - width, PITCH, lanes), jnp.float32)
@@ -60,13 +68,25 @@
     station = row & (PITCH - 1)
     target = jnp.where(row >= PITCH, station + width, station)
     chooser[...] = jnp.where((station < width) & (col == target), 1.0, 0.0).astype(jnp.bfloat16)
+    def spot(pair):
+        return pair + (PITCH - width) * (pair // width)
+
+    bases = [spot(128 * j) // 8 * 8 for j in range(tiles)] + [width * PITCH]
+    row = lax.broadcasted_iota(jnp.int32, (TALL, 128), 0).astype(jnp.float32)
+    for j in range(tiles):
+        pair = lax.broadcasted_iota(jnp.int32, (8, 128), 1).astype(jnp.float32) + 128.0 * j
+        first = jnp.floor((pair + 0.5) * (1.0 / width))
+        second = pair - first * width
+        goal = pair + (PITCH - width) * first - bases[j]
+        goal = jnp.where((first != second) & (first < width), goal, -1.0)
+        placer[j] = jnp.where(row == goal[0:1], 1.0, 0.0).astype(jnp.bfloat16)
     row = lax.broadcasted_iota(jnp.int32, (2 * lanes, lanes), 0) & (lanes - 1)
     col = lax.broadcasted_iota(jnp.int32, (2 * lanes, lanes), 1)
     half = dirs * channels
     same = ((row >= half) == (col >= half)) & ((row & (channels - 1)) == (col & (channels - 1)))
     mixer[...] = jnp.where(same, -1.0, 0.0).astype(jnp.bfloat16)
 
-    def window(first, second, i, start=None):
+    def window(first, second, i):
         offset = (2 * width * i) % 128
         if offset == 0:
             return first
@@ -74,8 +94,8 @@
         lane = lax.broadcasted_iota(jnp.int32, first.shape, 1)
         return jnp.where(lane < back, pltpu.roll(first, back, 1), pltpu.roll(second, back, 1))
 
-    def swung(right):
-        return lax.dot_general(chooser[...], right, (((1,), (1,)), ((), ())), preferred_element_type=jnp.float32)
+    def swung(left, right):
+        return lax.dot_general(left, right, (((1,), (1,)), ((), ())), preferred_element_type=jnp.float32)
 
     loads[0].wait()
     for part in range(2):
@@ -100,7 +120,7 @@
 
     for i in range(0, width // 2, 2):
         both = range(i, min(i + 2, width // 2))
-        turned = swung(jnp.concatenate([vis_side(k) for k in both], 0))
+        turned = swung(chooser[...], jnp.concatenate([vis_side(k) for k in both], 0))
         for n, k in enumerate(both):
             mine = turned[:, n * lanes : (n + 1) * lanes]
             vis[0, 2 * k : 2 * k + 2] = jnp.where(real, mine, 0.0).reshape(2, PITCH, lanes)
@@ -118,25 +138,29 @@
         cons[part, width:] = empty
         dual[part, width:] = empty
 
-    done = [0]
-
-    def turn(block):
-        pairs_to = range(block * GROUP // 2, min((block + 1) * GROUP // 2, width // 2))
-        last = min((2 * width * pairs_to[-1]) // 128 + 1, whole)
-        while done[0] <= last:
-            if done[0] < whole:
-                sky_loads[done[0]].wait()
-            else:
-                tail_load.wait()
-                sky_raw[whole, :, :, :, :, 0 : pairs - 128 * whole] = tail_raw[...]
-            done[0] += 1
-        for i in pairs_to:
-            j = (2 * width * i) // 128
-            turned = swung(window(sky_raw[j].reshape(2 * lanes, 128), sky_raw[j + 1].reshape(2 * lanes, 128), i))
+    for copy in sky_loads + [tail_load]:
+        copy.wait()
+    sky_raw[whole, :, :, :, :, 0 : pairs - 128 * whole] = tail_raw[...]
+    flat = sky.reshape(2, PITCH * PITCH, lanes)
+    sky_flat = sky_raw.reshape(tiles, 2 * lanes, 128)
+    state = {"tile": 0, "left": None}
+
+    def turn(limit):
+        while state["tile"] < tiles and bases[state["tile"]] < limit:
+            j = state["tile"]
+            turned = swung(placer[j], sky_flat[j])
+            size = bases[j + 1] - bases[j]
+            left = []
             for part in range(2):
-                sky[part, 2 * i : 2 * i + 2] = turned[:, part * lanes : (part + 1) * lanes].reshape(2, PITCH, lanes)
-                for p in (2 * i, 2 * i + 1):
-                    sky[part, p, p : p + 1] = jnp.zeros((1, lanes), jnp.float32)
+                mine = turned[:, part * lanes : (part + 1) * lanes]
+                head = mine[0:8]
+                if state["left"] is not None:
+                    head = head + state["left"][part]
+                flat[part, bases[j] : bases[j] + 8] = head
+                if size > 8:
+                    flat[part, bases[j] + 8 : bases[j + 1]] = mine[8:size]
+                left.append(mine[size : size + 8] if size + 8 <= TALL else None)
+            state["tile"], state["left"] = j + 1, left
 
     def parted(value):
         high = value.astype(jnp.bfloat16)
@@ -153,32 +177,37 @@
             ]
         return values[0]
 
-    def sweep(it, block, carry):
+    def front(it, block):
         gr, gi = gain[it, 0], gain[it, 1]
+        bank = block % 2
         sides = ([], [])
-        for b in range(GROUP):
+        here = min(GROUP, width - block * GROUP)
+        for b in range(here):
             p = block * GROUP + b
             sr, si = sky[0, p], sky[1, p]
             zr = sr * gr + si * gi
             zi = sr * gi - si * gr
-            z_keep[0, b] = zr
-            z_keep[1, b] = zi
-            lr, li = gain[it, 0, pl.ds(p, 1)], gain[it, 1, pl.ds(p, 1)]
+            z_keep[bank, 0, b] = zr
+            z_keep[bank, 1, b] = zi
+            lr, li = gain[it, 0, p : p + 1], gain[it, 1, p : p + 1]
             sides[0].append(parted(lr * zr + li * zi - vis[0, p]))
             sides[1].append(parted(li * zr - lr * zi - vis[1, p]))
         for part in range(2):
-            rest[part] = jnp.dot(
+            rest[bank, part, 0:here] = jnp.dot(
                 jnp.concatenate(sides[part], 0), mixer[...], preferred_element_type=jnp.float32
-            ).reshape(GROUP, PITCH, lanes)
-        sums_of = ([], [], [])
-        for b in range(GROUP):
-            zr, zi = z_keep[0, b], z_keep[1, b]
-            dr, di = rest[0, b], rest[1, b]
+            ).reshape(here, PITCH, lanes)
+
+    def back(block):
+        bank = block % 2
+        sums_of = [[], [], []]
+        for b in range(min(GROUP, width - block * GROUP)):
+            zr, zi = z_keep[bank, 0, b], z_keep[bank, 1, b]
+            dr, di = rest[bank, 0, b], rest[bank, 1, b]
             for i, value in enumerate((dr * zr - di * zi, dr * zi + di * zr, zr * zr + zi * zi)):
                 sums_of[i].append(jnp.sum(value.reshape(PITCH // 8, 8, lanes), 0))
         for i in range(3):
-            acc[i, pl.ds(pl.multiple_of(block * GROUP, GROUP), GROUP)] = gathered_rows(sums_of[i])
-        return carry
+            sums_of[i] += [jnp.zeros((8, lanes), jnp.float32)] * (GROUP - len(sums_of[i]))
+            acc[i, block * GROUP : (block + 1) * GROUP] = gathered_rows(sums_of[i])
 
     place = lax.broadcasted_iota(jnp.int32, (8, lanes), 1) & (channels - 1)
 
@@ -262,20 +291,24 @@
         for part in range(2):
             target[part] = jnp.transpose(state[part])[:, 0:width].reshape(pols, dirs, channels, width)
 
-    turn(0)
+    blocks = PITCH // GROUP
+    stops = {stop // GROUP - 1: chunk for chunk, (_, stop) in enumerate(CHUNKS)}
+    turn(GROUP * PITCH)
     for it in range(ITERS):
-        for chunk, (start, stop) in enumerate(CHUNKS):
+        front(it, 0)
+        for block in range(blocks):
             if it == 0:
-                for block in range(start // GROUP, stop // GROUP):
-                    if (block + 1) * GROUP < PITCH:
-                        turn(block + 1)
-                    sweep(it, block, 0)
-            else:
-                lax.fori_loop(start // GROUP, stop // GROUP, functools.partial(sweep, it), 0)
-                smooth(it - 1, chunk)
-            if it == 0 and chunk == 0:
-                pl.semaphore_wait(barrier, count - 1)
-            finish(it, chunk)
+                turn((block + 2) * GROUP * PITCH)
+            if block + 1 < blocks:
+                front(it, block + 1)
+            back(block)
+            if block in stops:
+                chunk = stops[block]
+                if it > 0:
+                    smooth(it - 1, chunk)
+                if it == 0 and chunk == 0:
+                    pl.semaphore_wait(barrier, count - 1)
+                finish(it, chunk)
     put(jones_out, gain.at[ITERS])
     for chunk in range(len(CHUNKS)):
         smooth(ITERS - 1, chunk)
@@ -360,11 +393,12 @@
                 pltpu.VMEM(duals_start.shape, f32),
                 pltpu.VMEM((2, 2 * channels, tiles * 128), f32),
                 pltpu.VMEM((2 * PITCH, 128), bf16),
+                pltpu.VMEM((tiles, TALL, 128), bf16),
                 pltpu.VMEM((2 * lanes, lanes), bf16),
                 pltpu.VMEM((2, PITCH, PITCH, lanes), f32),
                 pltpu.VMEM((2, PITCH, PITCH, lanes), f32),
-                pltpu.VMEM((2, GROUP, PITCH, lanes), f32),
-                pltpu.VMEM((2, GROUP, PITCH, lanes), f32),
+                pltpu.VMEM((2, 2, GROUP, PITCH, lanes), f32),
+                pltpu.VMEM((2, 2, GROUP, PITCH, lanes), f32),
                 pltpu.VMEM((3, PITCH, lanes), f32),
                 pltpu.VMEM((ITERS + 1,) + packed, f32),
                 pltpu.VMEM(packed, f32),

time: 23.3 us -> 22.6 us (0.970)
  Pallas kernels: 22.5 us -> 21.7 us
    pallas_call x1, Pallas kernels: 21.7 us -> 20.9 us  [local(): pl.pallas_call(functools.partial(kernel, count, (pols, dirs, channels, wi...]
where the time goes in v4:
time: 22.6 us; the launch traced here: 22.4 us
  Pallas kernels  21.7 us (96%)
  between operations  0.64 us (3%)
    pallas_call x1, Pallas kernels, local(): pl.pallas_call(functools.partial(kernel, count, (pols, dirs, channels, wi...  20.9 us
    pallas_call x1, Pallas kernels, local(): pl.pallas_call(deliver, out_shape=shapes, in_specs=[pl.BlockSpec(memory_s...  0.78 us

profile of v4, /device:TPU:0, one launch (start us, length us, event | category | flops | bytes accessed | tf_op | source)
XLA Modules:
  0.0 22.4 jit_solution(5870090044383993161)
XLA Ops:
  0.6 20.9 %shard_map.75 = (f32[2,2,16,4,62]{4,3,2,1,0:T(4,128)S(1)}, f32[2,2,16,4,62]{4,3,2,1,0:T(4,128)S(1)}, f32[2,2,16,4,62]{4,3,2,1,0:T(4,128)S(1)}, f32[2,2]{1,0:T(2,128)S(1)}) custom-call(f32[2,2,4,1,3844]{4,3,2,1,0:T(1,128)} %vis_in.1, bf16[2,2,16,4,3844]{4,3,2,1,0:T(4,128)(2,1)} %bitcast.1, f32[2,2,16,4,62]{4,3,2,1,0:T(4,128)} %jones_in.1, ...), custom_call_target="tpu_custom_call" | custom-call | tf_op jit(solution)/shard_map/pallas_call | solution.py:383
  21.6 0.8 %shard_map.76 = (f32[2,2,16,4,62]{4,3,2,1,0:T(4,128)}, f32[2,2,16,4,62]{4,3,2,1,0:T(4,128)}, f32[2,2,16,4,62]{4,3,2,1,0:T(4,128)}, f32[2,2]{1,0:T(2,128)}) custom-call(f32[2,2,16,4,62]{4,3,2,1,0:T(4,128)S(1)} %get-tuple-element.8.refs_0_, f32[2,2,16,4,62]{4,3,2,1,0:T(4,128)S(1)} %get-tuple-element.9.refs_1_, ...), custom_call_target="tpu_custom_call" | custom-call | tf_op jit(solution)/shard_map/pallas_call | solution.py:425

commit v5 on v4

--- a/solution.py
+++ b/solution.py
@@ -11,7 +11,8 @@
 PITCH = 64
 GROUP = 8
 TALL = 144
-CHUNKS = ((0, 32), (32, 56), (56, 64))
+HOLDS = (5, 7)
+CHUNKS = ((0, 32), (32, 64))
 MESH = pl.DeviceIdType.MESH
 
 penalty = 8.0
@@ -37,17 +38,18 @@
         pltpu.make_async_copy(source, target, load_sem.at[i])
         for i, (source, target) in enumerate(((vis_in, vis_raw), (jones_in, jones_raw), (duals_in, duals_raw)))
     ]
+    sky_rows = sky_in.reshape(2, pols, dirs * channels, pairs)
     sky_loads = [
-        pltpu.make_async_copy(sky_in.at[:, :, :, :, 128 * j : 128 * j + 128], sky_raw.at[j], sky_sem.at[j])
+        pltpu.make_async_copy(sky_rows.at[:, :, :, 128 * j : 128 * j + 128], sky_raw.at[j], sky_sem.at[j])
         for j in range(whole)
     ]
-    tail_load = pltpu.make_async_copy(sky_in.at[:, :, :, :, 128 * whole : pairs], tail_raw, tail_sem)
+    tail_load = pltpu.make_async_copy(sky_rows.at[:, :, :, 128 * whole : pairs], tail_raw, tail_sem)
     for copy in loads:
         copy.start()
 
     def issue(j, carry):
         start = pl.multiple_of(j * 128, 128)
-        pltpu.make_async_copy(sky_in.at[:, :, :, :, pl.ds(start, 128)], sky_raw.at[j], sky_sem.at[j]).start()
+        pltpu.make_async_copy(sky_rows.at[:, :, :, pl.ds(start, 128)], sky_raw.at[j], sky_sem.at[j]).start()
         return carry
 
     lax.fori_loop(0, whole, issue, 0)
@@ -60,8 +62,6 @@
         pl.semaphore_signal(barrier, inc=1, device_id={"chan": lax.rem(me + step, count)}, device_id_type=MESH)
     sums[...] = jnp.zeros_like(sums)
     sky_raw[whole] = jnp.zeros(sky_raw.shape[1:], sky_raw.dtype)
-    sky[:, width:] = jnp.zeros((2, PITCH - width, PITCH, lanes), jnp.float32)
-    vis[:, width:] = jnp.zeros((2, PITCH - width, PITCH, lanes), jnp.float32)
     vis_rows[:, :, 128 * whole :] = jnp.zeros((2, 2 * channels, 128 * (tiles - whole)), jnp.float32)
     row = lax.broadcasted_iota(jnp.int32, (2 * PITCH, 128), 0)
     col = lax.broadcasted_iota(jnp.int32, (2 * PITCH, 128), 1)
@@ -138,17 +138,23 @@
         cons[part, width:] = empty
         dual[part, width:] = empty
 
-    for copy in sky_loads + [tail_load]:
-        copy.wait()
-    sky_raw[whole, :, :, :, :, 0 : pairs - 128 * whole] = tail_raw[...]
+    state = {"tile": 0, "left": None, "have": 0}
+
+    def fetched(limit):
+        while state["have"] < min(limit, tiles):
+            if state["have"] < whole:
+                sky_loads[state["have"]].wait()
+            else:
+                tail_load.wait()
+                sky_raw[whole, :, :, :, 0 : pairs - 128 * whole] = tail_raw[...]
+            state["have"] += 1
+
     flat = sky.reshape(2, PITCH * PITCH, lanes)
-    sky_flat = sky_raw.reshape(tiles, 2 * lanes, 128)
-    state = {"tile": 0, "left": None}
 
     def turn(limit):
         while state["tile"] < tiles and bases[state["tile"]] < limit:
             j = state["tile"]
-            turned = swung(placer[j], sky_flat[j])
+            turned = swung(placer[j], sky_raw[j].reshape(2 * lanes, 128))
             size = bases[j + 1] - bases[j]
             left = []
             for part in range(2):
@@ -293,6 +299,7 @@
 
     blocks = PITCH // GROUP
     stops = {stop // GROUP - 1: chunk for chunk, (_, stop) in enumerate(CHUNKS)}
+    fetched(tiles)
     turn(GROUP * PITCH)
     for it in range(ITERS):
         front(it, 0)
@@ -302,13 +309,15 @@
             if block + 1 < blocks:
                 front(it, block + 1)
             back(block)
-            if block in stops:
-                chunk = stops[block]
-                if it > 0:
-                    smooth(it - 1, chunk)
-                if it == 0 and chunk == 0:
+            if it == 0 and block in stops:
+                if stops[block] == 0:
                     pl.semaphore_wait(barrier, count - 1)
-                finish(it, chunk)
+                finish(it, stops[block])
+            if it > 0:
+                for chunk, hold in enumerate(HOLDS):
+                    if block == hold:
+                        smooth(it - 1, chunk)
+                        finish(it, chunk)
     put(jones_out, gain.at[ITERS])
     for chunk in range(len(CHUNKS)):
         smooth(ITERS - 1, chunk)
@@ -387,8 +396,8 @@
             out_specs=tuple([pl.BlockSpec(memory_space=pltpu.VMEM)] * 4),
             scratch_shapes=[
                 pltpu.VMEM(visibility.shape, f32),
-                pltpu.VMEM((tiles, 2, pols, dirs, channels, 128), bf16),
-                pltpu.VMEM((2, pols, dirs, channels, pairs - 128 * whole), bf16),
+                pltpu.VMEM((tiles, 2, pols, dirs * channels, 128), bf16),
+                pltpu.VMEM((2, pols, dirs * channels, pairs - 128 * whole), bf16),
                 pltpu.VMEM(jones_start.shape, f32),
                 pltpu.VMEM(duals_start.shape, f32),
                 pltpu.VMEM((2, 2 * channels, tiles * 128), f32),

time: 22.6 us -> 21.7 us (0.960)
  Pallas kernels: 21.7 us -> 20.9 us
    pallas_call x1, Pallas kernels: 20.9 us -> 20.1 us  [local(): pl.pallas_call(functools.partial(kernel, count, (pols, dirs, channels, wi...]
where the time goes in v5:
time: 21.7 us; the launch traced here: 21.5 us
  Pallas kernels  20.9 us (96%)
  between operations  0.64 us (3%)
    pallas_call x1, Pallas kernels, local(): pl.pallas_call(functools.partial(kernel, count, (pols, dirs, channels, wi...  20.1 us
    pallas_call x1, Pallas kernels, local(): pl.pallas_call(deliver, out_shape=shapes, in_specs=[pl.BlockSpec(memory_s...  0.78 us

profile of v5, /device:TPU:0, one launch (start us, length us, event | category | flops | bytes accessed | tf_op | source)
XLA Modules:
  0.0 21.5 jit_solution(45082048771430109)
XLA Ops:
  0.6 20.1 %shard_map.75 = (f32[2,2,16,4,62]{4,3,2,1,0:T(4,128)S(1)}, f32[2,2,16,4,62]{4,3,2,1,0:T(4,128)S(1)}, f32[2,2,16,4,62]{4,3,2,1,0:T(4,128)S(1)}, f32[2,2]{1,0:T(2,128)S(1)}) custom-call(f32[2,2,4,1,3844]{4,3,2,1,0:T(1,128)} %vis_in.1, bf16[2,2,16,4,3844]{4,3,2,1,0:T(4,128)(2,1)} %bitcast.1, f32[2,2,16,4,62]{4,3,2,1,0:T(4,128)} %jones_in.1, ...), custom_call_target="tpu_custom_call" | custom-call | tf_op jit(solution)/shard_map/pallas_call | solution.py:392
  20.7 0.8 %shard_map.76 = (f32[2,2,16,4,62]{4,3,2,1,0:T(4,128)}, f32[2,2,16,4,62]{4,3,2,1,0:T(4,128)}, f32[2,2,16,4,62]{4,3,2,1,0:T(4,128)}, f32[2,2]{1,0:T(2,128)}) custom-call(f32[2,2,16,4,62]{4,3,2,1,0:T(4,128)S(1)} %get-tuple-element.8.refs_0_, f32[2,2,16,4,62]{4,3,2,1,0:T(4,128)S(1)} %get-tuple-element.9.refs_1_, ...), custom_call_target="tpu_custom_call" | custom-call | tf_op jit(solution)/shard_map/pallas_call | solution.py:434

commit v6 on v5

--- a/solution.py
+++ b/solution.py
@@ -247,10 +247,10 @@
     def finish(it, chunk):
         rows = slice(*CHUNKS[chunk])
         lower = acc[2, rows]
-        scale = lower + penalty
+        scale = 1.0 / (lower + penalty)
         for part in range(2):
             goal = cons[part, rows] - dual[part, rows]
-            fresh = (acc[part, rows] + gain[it, part, rows] * lower + penalty * goal) / scale
+            fresh = (acc[part, rows] + gain[it, part, rows] * lower + penalty * goal) * scale
             gain[it + 1, part, rows] = fresh
             summed[it, part, rows] = fresh + dual[part, rows]
 
@@ -264,6 +264,7 @@
 
     def smooth(it, chunk):
         rows = slice(*CHUNKS[chunk])
+        own = [mixed(summed[it, part, rows], 0) for part in range(2)]
 
         @pl.when(me > 0)
         def _():
@@ -275,7 +276,7 @@
 
         for part in range(2):
             fresh = (
-                mixed(summed[it, part, rows], 0)
+                own[part]
                 + mixed(from_low[it, part, rows], -channels)
                 + mixed(from_high[it, part, rows], channels)
             )
@@ -299,8 +300,9 @@
 
     blocks = PITCH // GROUP
     stops = {stop // GROUP - 1: chunk for chunk, (_, stop) in enumerate(CHUNKS)}
+    fetched(10)
+    turn(2 * GROUP * PITCH)
     fetched(tiles)
-    turn(GROUP * PITCH)
     for it in range(ITERS):
         front(it, 0)
         for block in range(blocks):
@@ -351,7 +353,9 @@
                 down_copy(it, chunk).wait_send()
 
     for step in range(1, count):
-        norm_copy(step).wait()
+        norm_copy(step).wait_send()
+    for step in range(1, count):
+        norm_copy(step).wait_recv()
     gathered = slots[0]
     for j in range(1, count):
         gathered = gathered + slots[j]

time: 21.7 us -> 21.4 us (0.986)
  no operation moved by 1% of the time
where the time goes in v6:
time: 21.4 us; the launch traced here: 21.3 us
  Pallas kernels  20.7 us (97%)
  between operations  0.64 us (3%)
    pallas_call x1, Pallas kernels, local(): pl.pallas_call(functools.partial(kernel, count, (pols, dirs, channels, wi...  19.9 us
    pallas_call x1, Pallas kernels, local(): pl.pallas_call(deliver, out_shape=shapes, in_specs=[pl.BlockSpec(memory_s...  0.78 us

profile of v6, /device:TPU:0, one launch (start us, length us, event | category | flops | bytes accessed | tf_op | source)
XLA Modules:
  0.0 21.3 jit_solution(1831529538005818031)
XLA Ops:
  0.6 19.9 %shard_map.75 = (f32[2,2,16,4,62]{4,3,2,1,0:T(4,128)S(1)}, f32[2,2,16,4,62]{4,3,2,1,0:T(4,128)S(1)}, f32[2,2,16,4,62]{4,3,2,1,0:T(4,128)S(1)}, f32[2,2]{1,0:T(2,128)S(1)}) custom-call(f32[2,2,4,1,3844]{4,3,2,1,0:T(1,128)} %vis_in.1, bf16[2,2,16,4,3844]{4,3,2,1,0:T(4,128)(2,1)} %bitcast.1, f32[2,2,16,4,62]{4,3,2,1,0:T(4,128)} %jones_in.1, ...), custom_call_target="tpu_custom_call" | custom-call | tf_op jit(solution)/shard_map/pallas_call | solution.py:396
  20.5 0.8 %shard_map.76 = (f32[2,2,16,4,62]{4,3,2,1,0:T(4,128)}, f32[2,2,16,4,62]{4,3,2,1,0:T(4,128)}, f32[2,2,16,4,62]{4,3,2,1,0:T(4,128)}, f32[2,2]{1,0:T(2,128)}) custom-call(f32[2,2,16,4,62]{4,3,2,1,0:T(4,128)S(1)} %get-tuple-element.8.refs_0_, f32[2,2,16,4,62]{4,3,2,1,0:T(4,128)S(1)} %get-tuple-element.9.refs_1_, ...), custom_call_target="tpu_custom_call" | custom-call | tf_op jit(solution)/shard_map/pallas_call | solution.py:438

commit v7 on v6

--- a/solution.py
+++ b/solution.py
@@ -320,7 +320,6 @@
                     if block == hold:
                         smooth(it - 1, chunk)
                         finish(it, chunk)
-    put(jones_out, gain.at[ITERS])
     for chunk in range(len(CHUNKS)):
         smooth(ITERS - 1, chunk)
 
@@ -338,6 +337,7 @@
     slots[pl.ds(me, 1)] = packed[None]
     for step in range(1, count):
         norm_copy(step).start()
+    put(jones_out, gain.at[ITERS])
     put(consensus_out, cons)
     put(duals_out, dual)
 

time: 21.4 us -> 21.4 us (level)
  no operation moved by 1% of the time
where the time goes in v7:
time: 21.4 us; the launch traced here: 21.3 us
  Pallas kernels  20.7 us (97%)
  between operations  0.64 us (3%)
    pallas_call x1, Pallas kernels, local(): pl.pallas_call(functools.partial(kernel, count, (pols, dirs, channels, wi...  19.9 us
    pallas_call x1, Pallas kernels, local(): pl.pallas_call(deliver, out_shape=shapes, in_specs=[pl.BlockSpec(memory_s...  0.78 us

profile of v7, /device:TPU:0, one launch (start us, length us, event | category | flops | bytes accessed | tf_op | source)
XLA Modules:
  0.0 21.3 jit_solution(16719643121498252097)
XLA Ops:
  0.6 19.9 %shard_map.75 = (f32[2,2,16,4,62]{4,3,2,1,0:T(4,128)S(1)}, f32[2,2,16,4,62]{4,3,2,1,0:T(4,128)S(1)}, f32[2,2,16,4,62]{4,3,2,1,0:T(4,128)S(1)}, f32[2,2]{1,0:T(2,128)S(1)}) custom-call(f32[2,2,4,1,3844]{4,3,2,1,0:T(1,128)} %vis_in.1, bf16[2,2,16,4,3844]{4,3,2,1,0:T(4,128)(2,1)} %bitcast.1, f32[2,2,16,4,62]{4,3,2,1,0:T(4,128)} %jones_in.1, ...), custom_call_target="tpu_custom_call" | custom-call | tf_op jit(solution)/shard_map/pallas_call | solution.py:396
  20.5 0.8 %shard_map.76 = (f32[2,2,16,4,62]{4,3,2,1,0:T(4,128)}, f32[2,2,16,4,62]{4,3,2,1,0:T(4,128)}, f32[2,2,16,4,62]{4,3,2,1,0:T(4,128)}, f32[2,2]{1,0:T(2,128)}) custom-call(f32[2,2,16,4,62]{4,3,2,1,0:T(4,128)S(1)} %get-tuple-element.8.refs_0_, f32[2,2,16,4,62]{4,3,2,1,0:T(4,128)S(1)} %get-tuple-element.9.refs_1_, ...), custom_call_target="tpu_custom_call" | custom-call | tf_op jit(solution)/shard_map/pallas_call | solution.py:438
